TPU v7x, 256 devices: a whole 4x4x8 slice. The times are simulated.
256 devices in a mesh: lat: 16 (over z, core), rad: 16 (over x, y).
Axes of the slice: x: 4, y: 4, z: 8, core: 2. Of those that a mesh axis runs over, the one named last changes fastest.
Arguments:
- residual: float32 [3, 128, 128, 256], P(None, 'rad', 'lat'), may hold values from -30 to 30
- prev_basis: float32 [4, 3, 128, 128, 256], P(None, None, 'rad', 'lat'), may hold values from -30 to 30
- layer_ids: int32 [64, 64, 128], P('rad', 'lat'), may hold values from 0 to 7
- viscosity: float32 [8], replicated, may hold values from 0.1 to 1
- shifts: float32 [4], replicated, may hold values from 0.3 to 2
Outputs:
- new_basis: float32 [4, 3, 128, 128, 256], P(None, None, 'rad', 'lat')
- gram_matrix: float32 [9, 9], replicated
All inputs are finite; a program needn't handle non-finite values.
Results may differ from a plain program's by a relative error of at most 0.00019.
Values sent between devices are 32-bit elements; how exact they have to be, the bound alone decides.
A program may use at most 128 MiB of HBM per device.

v0:
```python
import functools

import jax
import jax.numpy as jnp
from jax import lax
from jax.experimental import pallas as pl
from jax.experimental.pallas import tpu as pltpu
from jax.sharding import PartitionSpec as P

MESH = pl.DeviceIdType.MESH
HIGHEST = lax.Precision.HIGHEST
DEPTH = 2
MASS = (1.0 / 36.0, 1.0 / 12.0, 1.0 / 45.0)
STIFF = (0.0, 1.0, 4.0 / 3.0)
DIRECTIONS = [(dr, dl) for dr in (-1, 1, 0) for dl in (-1, 1, 0) if (dr, dl) != (0, 0)]


def mode_weight(i, j, k):
    return (
        STIFF[i] * MASS[j] * MASS[k]
        + MASS[i] * STIFF[j] * MASS[k]
        + MASS[i] * MASS[j] * STIFF[k]
    )


def to_modes(a, b, c):
    double = b + b
    ends = a + c
    return ends + (double + double), a - c, ends - double


def from_modes(g0, g1, g2):
    ends = g0 + g2
    half = (g0 + g0) - g2
    return ends + g1, half + half, ends - g1


def kernel(
    n_steps, n_prev, n_layers, n_rad, n_lat, dof_count,
    residual, prev_basis, layer_ids, viscosity, shifts,
    new_basis, gram,
    res_v, prev_v, ids_v, pick, pick_t, field, prev_d, wide, parts, pack, side, eta, eta_wide,
    out_v, rows, row_lat, row_rad,
    in_sem, out_sem, send_sem, recv_sem, esend_sem, erecv_sem, gsend_sem, grecv_sem,
):
    rad = lax.axis_index("rad")
    lat = lax.axis_index("lat")
    n_exchange = n_steps // DEPTH
    up = 2 * DEPTH
    down = 2 * DEPTH - 1

    copies = [
        pltpu.make_async_copy(residual, res_v, in_sem.at[0]),
        pltpu.make_async_copy(layer_ids, ids_v, in_sem.at[1]),
        pltpu.make_async_copy(prev_basis, prev_v, in_sem.at[2]),
    ]
    for copy in copies:
        copy.start()

    barrier = pltpu.get_barrier_semaphore()

    def here(dr, dl):
        inside = None
        for value, step, count in ((rad, dr, n_rad), (lat, dl, n_lat)):
            if step:
                test = value < count - 1 if step > 0 else value > 0
                inside = test if inside is None else jnp.logical_and(inside, test)
        return inside

    for d in range(1, n_lat):
        pl.semaphore_signal(
            barrier, inc=1, device_id={"lat": lax.rem(lat + d, n_lat), "rad": rad}, device_id_type=MESH
        )
    for d in range(1, n_rad):
        pl.semaphore_signal(
            barrier, inc=1, device_id={"lat": lat, "rad": lax.rem(rad + d, n_rad)}, device_id_type=MESH
        )
    for dr in (-1, 1):
        for dl in (-1, 1):

            @pl.when(here(dr, dl))
            def _():
                pl.semaphore_signal(
                    barrier, inc=1, device_id={"lat": lat + dl, "rad": rad + dr}, device_id_type=MESH
                )

    rows[...] = jnp.zeros(rows.shape, jnp.float32)
    sub = lax.broadcasted_iota(jnp.int32, (8, 128), 0)
    lane = lax.broadcasted_iota(jnp.int32, (8, 128), 1)
    upper_rows = sub < 4

    row_id = lax.broadcasted_iota(jnp.int32, (256, 256), 0)
    col_id = lax.broadcasted_iota(jnp.int32, (256, 256), 1)
    pick[...] = (row_id == jnp.where(col_id < 128, 2 * col_id, 2 * col_id - 255)).astype(jnp.float32)
    pick_t[...] = (col_id == jnp.where(row_id < 128, 2 * row_id, 2 * row_id - 255)).astype(jnp.float32)

    def split_y(values, store):
        split = jnp.dot(
            values.reshape(192, 256), pick[...], precision=HIGHEST, preferred_element_type=jnp.float32
        )
        for c in range(3):
            block = split[c * 64 : (c + 1) * 64]
            store(0, c, block[:, :128].reshape(8, 8, 128))
            store(1, c, block[:, 128:].reshape(8, 8, 128))

    copies[0].wait()

    def store_field(y, c, value):
        field[0, 4:12, y, c] = value

    split_y(res_v[...], store_field)

    copies[1].wait()
    for a in range(4):
        ids = ids_v[a]
        values = jnp.zeros(ids.shape, jnp.float32)
        for layer in range(n_layers):
            values = jnp.where(ids == layer, viscosity[layer], values)
        eta[1, 2 + a] = jnp.concatenate([values, values], axis=0)

    def pack_sides(e, k):
        for p in range(8):
            for c in range(3):
                even = field[k, 4 + p, 0, c]
                odd = field[k, 4 + p, 1, c]
                pack[e, 0, p, c] = jnp.where(upper_rows, even, pltpu.roll(odd, 4, 0))
                pack[e, 1, p, c] = jnp.where(upper_rows, pltpu.roll(even, 4, 0), odd)

    def halo_copy(e, n):
        dr, dl = DIRECTIONS[n]
        k = e * DEPTH
        source, target, size = {
            1: (8 - up, 4 - up, up), -1: (0, 12, down), 0: (0, 4, 8)
        }[dr]
        if dl == 0:
            src = field.at[k, pl.ds(4 + source, size)]
            dst = field.at[k, pl.ds(target, size)]
        else:
            src = pack.at[e, 0 if dl < 0 else 1, pl.ds(source, size)]
            dst = side.at[e, 1 if dl < 0 else 0, pl.ds(target, size)]
        return pltpu.make_async_remote_copy(
            src_ref=src, dst_ref=dst, send_sem=send_sem.at[e, n], recv_sem=recv_sem.at[e, n],
            device_id={"lat": lat + dl, "rad": rad + dr}, device_id_type=MESH,
        )

    def eta_copy(n):
        dr, dl = DIRECTIONS[n]
        source, target, size = {1: (2, 0, 2), -1: (0, 6, 2), 0: (0, 2, 4)}[dr]
        return pltpu.make_async_remote_copy(
            src_ref=eta.at[1, pl.ds(2 + source, size)],
            dst_ref=eta.at[1 - dl, pl.ds(target, size)],
            send_sem=esend_sem.at[n], recv_sem=erecv_sem.at[n],
            device_id={"lat": lat + dl, "rad": rad + dr}, device_id_type=MESH,
        )

    def each_direction(receive, act):
        for n, (dr, dl) in enumerate(DIRECTIONS):
            test = here(-dr, -dl) if receive else here(dr, dl)

            @pl.when(test)
            def _():
                act(n)

    def widen(p, c, tile, even, odd):
        after = jnp.where(lane < 127, pltpu.roll(even, 127, 1), 0.0)
        for slot, value in enumerate((even, odd, after)):
            wide[p, slot, c, tile * 8 : tile * 8 + 8] = value
            if tile == 0:
                wide[p, slot, c, 16:24] = value

    def widen_own(k, planes):
        for p in planes:
            for c in range(3):
                widen(p, c, 0, field[k, p, 0, c], field[k, p, 1, c])

    def widen_sides(e, planes):
        for p in planes:
            for c in range(3):
                below = side[e, 0, p, c]
                above = side[e, 1, p, c]
                widen(
                    p, c, 1,
                    jnp.where(upper_rows, above, pltpu.roll(below, 4, 0)),
                    jnp.where(upper_rows, pltpu.roll(above, 4, 0), below),
                )

    def dots(n):
        def tile(m, p, y, c):
            return prev_d[m, p, y, c] if m < n_prev else field[m - n_prev, 4 + p, y, c]

        def body(p, sums):
            sums = list(sums)
            for y in range(2):
                for c in range(3):
                    new = tile(n, p, y, c)
                    for m in range(n + 1):
                        other = new if m == n else tile(m, p, y, c)
                        sums[m] = sums[m] + new * other
            return tuple(sums)

        zero = jnp.zeros((8, 128), jnp.float32)
        sums = lax.fori_loop(0, 8, body, (zero,) * (n + 1))
        width = n_prev + n_steps + 1
        for m in range(n + 1):
            total = jnp.sum(sums[m], axis=0, keepdims=True)
            rows[n * width + m : n * width + m + 1] = total
            if m != n:
                rows[m * width + n : m * width + n + 1] = total

    def planes_modes(p, c):
        nodes = [
            [wide[p, slot, c, pl.ds(start, 8, stride=2)] for start in range(3)] for slot in range(3)
        ]
        lines = [to_modes(*nodes[slot]) for slot in range(3)]
        return [to_modes(lines[0][i], lines[1][i], lines[2][i]) for i in range(3)]

    def put_plane(p, c, modes):
        lines = [from_modes(*modes[i]) for i in range(3)]
        for slot in range(3):
            low, mid, high = from_modes(lines[0][slot], lines[1][slot], lines[2][slot])
            parts[p, slot, c, pl.ds(0, 8, stride=2)] = low + pltpu.roll(high, 1, 0)
            parts[p, slot, c, pl.ds(1, 8, stride=2)] = mid

    def apply(first, last, low_plane, high_plane):
        def body(c, nothing):
            below = planes_modes(2 * first, c)
            carried = None
            for a in range(first, last):
                visc = eta_wide[a]
                weight = {}
                for i in range(3):
                    for j in range(i, 3):
                        for l in range(j, 3):
                            if l > 0:
                                weight[i, j, l] = visc * mode_weight(i, j, l)
                middle = planes_modes(2 * a + 1, c)
                above = planes_modes(2 * a + 2, c)
                at_low = [[None] * 3 for _ in range(3)]
                at_mid = [[None] * 3 for _ in range(3)]
                at_high = [[None] * 3 for _ in range(3)]
                for i in range(3):
                    for j in range(3):
                        m = to_modes(below[i][j], middle[i][j], above[i][j])
                        g = [
                            None if i + j + l == 0 else m[l] * weight[tuple(sorted((i, j, l)))]
                            for l in range(3)
                        ]
                        if g[0] is None:
                            twice = g[2] + g[2]
                            out = (g[2] + g[1], -twice, g[2] - g[1])
                        else:
                            out = from_modes(*g)
                        at_low[i][j] = out[0] if carried is None else out[0] + carried[i][j]
                        at_mid[i][j] = out[1]
                        at_high[i][j] = out[2]
                if low_plane <= 2 * a <= high_plane:
                    put_plane(2 * a, c, at_low)
                if low_plane <= 2 * a + 1 <= high_plane:
                    put_plane(2 * a + 1, c, at_mid)
                carried = at_high
                below = above
            return nothing

        lax.fori_loop(0, 3, body, 0)

    keep_rad = jnp.where(rad == n_rad - 1, 0.0, 1.0)
    keep_lat = jnp.where(jnp.logical_and(upper_rows, lat == n_lat - 1), 0.0, 1.0)

    def advance(k, planes, tiles, outer):
        shift = shifts[k]
        for p in planes:
            for c in range(3):
                for tile in tiles:
                    at = slice(tile * 8, tile * 8 + 8)
                    moved = jnp.where(lane > 0, pltpu.roll(parts[p, 2, c, at], 1, 1), 0.0)
                    even = parts[p, 0, c, at] + moved - shift * wide[p, 0, c, at]
                    odd = parts[p, 1, c, at] - shift * wide[p, 1, c, at]
                    if p >= 12:
                        even = even * keep_rad
                        odd = odd * keep_rad
                    if tile == 1:
                        even = even * keep_lat
                        odd = odd * keep_lat
                    if tile == 0 and 4 <= p < 12:
                        field[k + 1, p, 0, c] = even
                        field[k + 1, p, 1, c] = odd
                    if outer:
                        widen(p, c, tile, even, odd)

    def put_out(k):
        lines = []
        for c in range(3):
            even = field[k + 1, 4:12, 0, c].reshape(64, 128)
            odd = field[k + 1, 4:12, 1, c].reshape(64, 128)
            lines.append(jnp.concatenate([even, odd], axis=1))
        merged = jnp.dot(
            jnp.concatenate(lines, axis=0), pick_t[...],
            precision=HIGHEST, preferred_element_type=jnp.float32,
        )
        out_v[k] = merged.reshape(3, 8, 8, 256)
        pltpu.make_async_copy(out_v.at[k], new_basis.at[k], out_sem.at[k]).start()

    def zero_edges():
        blank = jnp.zeros((8, 128), jnp.float32)

        @pl.when(rad == 0)
        def _():
            for e in range(n_exchange):
                field[e * DEPTH, 4 - up : 4] = jnp.broadcast_to(blank, (up, 2, 3, 8, 128))
                side[e, :, 4 - up : 4] = jnp.broadcast_to(blank, (2, up, 3, 8, 128))
            eta[:, 0:2] = jnp.broadcast_to(blank, (3, 2, 8, 128))

        @pl.when(rad == n_rad - 1)
        def _():
            for e in range(n_exchange):
                field[e * DEPTH, 12 : 12 + down] = jnp.broadcast_to(blank, (down, 2, 3, 8, 128))
                side[e, :, 12 : 12 + down] = jnp.broadcast_to(blank, (2, down, 3, 8, 128))
            eta[:, 6:8] = jnp.broadcast_to(blank, (3, 2, 8, 128))

        @pl.when(lat == 0)
        def _():
            for e in range(n_exchange):
                side[e, 0] = jnp.broadcast_to(blank, (16, 3, 8, 128))
            eta[0] = jnp.broadcast_to(blank, (8, 8, 128))

        @pl.when(lat == n_lat - 1)
        def _():
            for e in range(n_exchange):
                side[e, 1] = jnp.broadcast_to(blank, (16, 3, 8, 128))
            eta[2] = jnp.broadcast_to(blank, (8, 8, 128))

    pack_sides(0, 0)
    corners = 0
    for dr in (-1, 1):
        for dl in (-1, 1):
            corners = corners + jnp.where(here(dr, dl), 1, 0)
    pl.semaphore_wait(barrier, n_lat + n_rad - 2 + corners)

    for e in range(n_exchange):
        k = e * DEPTH
        if e == 0:
            each_direction(False, lambda n: eta_copy(n).start())
        each_direction(False, lambda n: halo_copy(e, n).start())
        if e == 0:
            zero_edges()
            widen_own(0, range(4, 12))
            copies[2].wait()
            for m in range(n_prev):

                def store_prev(y, c, value):
                    prev_d[m, :, y, c] = value

                split_y(prev_v[m], store_prev)
            for m in range(n_prev + 1):
                dots(m)
        else:
            for j in range(k - DEPTH + 1, k + 1):
                dots(n_prev + j)
                put_out(j - 1)
        if e == 0:
            each_direction(True, lambda n: eta_copy(n).wait_recv())
            for a in range(8):
                eta_wide[a] = jnp.where(
                    upper_rows, eta[1, a], jnp.where(sub < 6, eta[2, a], eta[0, a])
                )
        each_direction(True, lambda n: halo_copy(e, n).wait_recv())
        low, high = 4 - up, 12 + down
        widen_own(k, list(range(low, 4)) + list(range(12, high)))
        widen_sides(e, range(low, high))
        for step in range(DEPTH):
            left = DEPTH - 1 - step
            apply(1 - left, 6 + left, 4 - 2 * left, 11 + left)
            last = step == DEPTH - 1
            advance(
                k + step, range(4 - 2 * left, 12 + left), (0,) if last else (0, 1),
                not last or e < n_exchange - 1,
            )
        if e < n_exchange - 1:
            pack_sides(e + 1, k + DEPTH)

    for j in range(n_steps - DEPTH + 1, n_steps + 1):
        dots(n_prev + j)
    ones = jnp.ones((8, 128), jnp.float32)
    local = lax.dot_general(
        ones, rows[...], (((1,), (1,)), ((), ())), precision=HIGHEST, preferred_element_type=jnp.float32
    )
    row_lat[lat] = local[0:1]

    def row_copy(stage, d):
        buffer, me, count = (row_lat, lat, n_lat) if stage == 0 else (row_rad, rad, n_rad)
        peer = lax.rem(me + d, count)
        target = {"lat": peer, "rad": rad} if stage == 0 else {"lat": lat, "rad": peer}
        return pltpu.make_async_remote_copy(
            src_ref=buffer.at[me], dst_ref=buffer.at[me],
            send_sem=gsend_sem.at[stage, d], recv_sem=grecv_sem.at[stage, d],
            device_id=target, device_id_type=MESH,
        )

    for d in range(1, n_lat):
        row_copy(0, d).start()
    for j in range(n_steps - DEPTH + 1, n_steps + 1):
        put_out(j - 1)
    for d in range(1, n_lat):
        row_copy(0, d).wait_recv()
    total = row_lat[0]
    for d in range(1, n_lat):
        total = total + row_lat[d]
    row_rad[rad] = total
    for d in range(1, n_rad):
        row_copy(1, d).start()
    for k in range(n_steps):
        pltpu.make_async_copy(out_v.at[k], new_basis.at[k], out_sem.at[k]).wait()
    each_direction(False, lambda n: eta_copy(n).wait_send())
    for e in range(n_exchange):
        each_direction(False, lambda n: halo_copy(e, n).wait_send())
    for d in range(1, n_lat):
        row_copy(0, d).wait_send()
    for d in range(1, n_rad):
        row_copy(1, d).wait_recv()
    total = row_rad[0]
    for d in range(1, n_rad):
        total = total + row_rad[d]
    total = total * (1.0 / dof_count)
    width = n_prev + n_steps + 1
    for i in range(width):
        line = total if i == 0 else pltpu.roll(jnp.broadcast_to(total, (8, 128)), 128 - i * width, 1)[0:1]
        gram[i : i + 1, :] = line[:, :width]
    for d in range(1, n_rad):
        row_copy(1, d).wait_send()


def solution(mesh):
    n_lat = mesh.shape["lat"]
    n_rad = mesh.shape["rad"]

    def on_device(residual, prev_basis, layer_ids, viscosity, shifts):
        n_steps = shifts.shape[0]
        n_prev = prev_basis.shape[0]
        width = n_prev + n_steps + 1
        n_exchange = n_steps // DEPTH
        dof_count = residual.size * n_lat * n_rad
        f32 = jnp.float32
        dma = pltpu.SemaphoreType.DMA
        return pl.pallas_call(
            functools.partial(
                kernel, n_steps, n_prev, viscosity.shape[0], n_rad, n_lat, dof_count
            ),
            out_shape=(
                jax.ShapeDtypeStruct((n_steps,) + residual.shape, f32),
                jax.ShapeDtypeStruct((width, width), f32),
            ),
            in_specs=[pl.BlockSpec(memory_space=pl.ANY)] * 3
            + [pl.BlockSpec(memory_space=pltpu.SMEM)] * 2,
            out_specs=(
                pl.BlockSpec(memory_space=pl.ANY),
                pl.BlockSpec(memory_space=pltpu.VMEM),
            ),
            scratch_shapes=[
                pltpu.VMEM(residual.shape, f32),
                pltpu.VMEM(prev_basis.shape, f32),
                pltpu.VMEM(layer_ids.shape, jnp.int32),
                pltpu.VMEM((256, 256), f32),
                pltpu.VMEM((256, 256), f32),
                pltpu.VMEM((n_steps + 1, 16, 2, 3, 8, 128), f32),
                pltpu.VMEM((n_prev, 8, 2, 3, 8, 128), f32),
                pltpu.VMEM((16, 3, 3, 24, 128), f32),
                pltpu.VMEM((16, 3, 3, 16, 128), f32),
                pltpu.VMEM((n_exchange, 2, 8, 3, 8, 128), f32),
                pltpu.VMEM((n_exchange, 2, 16, 3, 8, 128), f32),
                pltpu.VMEM((3, 8, 8, 128), f32),
                pltpu.VMEM((8, 8, 128), f32),
                pltpu.VMEM((n_steps,) + residual.shape, f32),
                pltpu.VMEM((128, 128), f32),
                pltpu.VMEM((n_lat, 1, 128), f32),
                pltpu.VMEM((n_rad, 1, 128), f32),
                dma((3,)),
                dma((n_steps,)),
                dma((n_exchange, 8)),
                dma((n_exchange, 8)),
                dma((8,)),
                dma((8,)),
                dma((2, max(n_lat, n_rad))),
                dma((2, max(n_lat, n_rad))),
            ],
            compiler_params=pltpu.CompilerParams(collective_id=0, has_side_effects=True),
        )(residual, prev_basis, layer_ids, viscosity, shifts)

    placed = (P(None, "rad", "lat", None), P(None, None, "rad", "lat", None), P("rad", "lat", None), P(), P())
    return jax.shard_map(
        on_device,
        mesh=mesh,
        in_specs=placed,
        out_specs=(P(None, None, "rad", "lat", None), P()),
        check_vma=False,
    )
```

profile of v0, /device:TPU:1, one launch (start us, length us, event | category | flops | bytes accessed | tf_op | source)
XLA Modules:
  0.0 41.8 jit_solution(7506192163148200790)
XLA Ops:
  0.6 38.5 %shard_map.68 = (f32[4,3,8,8,256]{4,3,2,1,0:T(8,128)}, f32[9,9]{1,0:T(8,128)}) custom-call(f32[3,8,8,256]{3,2,1,0:T(8,128)} %residual.1, f32[4,3,8,8,256]{4,3,2,1,0:T(8,128)} %prev_basis.1, s32[4,4,128]{2,1,0:T(4,128)} %layer_ids.1, f32[8]{0:T(128)} %viscosity.1, f32[4]{0:T(128)} %shifts.1), custom_call_target="tpu_custom_call" | custom-call | tf_op jit(solution)/shard_map/pallas_call | solution.py:444
  39.1 0.0 copy-start
  39.1 2.1 %copy.9 = f32[4,3,8,8,256]{4,3,2,1,0:T(8,128)} copy(f32[4,3,8,8,256]{4,3,2,1,0:T(8,128)} %get-tuple-element.4) | data formatting | bytes 1572864
  41.2 0.0 copy-done
  41.2 0.6 %copy.10 = f32[9,9]{1,0:T(8,128)} copy(f32[9,9]{1,0:T(8,128)S(1)} %copy-done) | data formatting | bytes 648
Async XLA Ops:
  39.1 2.1 %copy-start = (f32[9,9]{1,0:T(8,128)S(1)}, f32[9,9]{1,0:T(8,128)}, u32[]{:S(2)}) copy-start(f32[9,9]{1,0:T(8,128)} %get-tuple-element.5) | copy-start | bytes 976
where the time goes:
time: 41.9 us; the launch traced here: 41.8 us
  Pallas kernels  38.5 us (92%)
  local copies, waits for them, and re-layouts  2.67 us (6%)
  between operations  0.65 us (2%)
    pallas_call x1, Pallas kernels, on_device(): pl.pallas_call(functools.partial(kernel, n_steps, n_prev, viscosity.shape...  38.5 us
    unnamed x4, local copies, waits for them, and re-layouts  2.67 us

commit v1 on v0

v1 whole, which is shorter than its diff:
```python
import functools

import jax
import jax.numpy as jnp
from jax import lax
from jax.experimental import pallas as pl
from jax.experimental.pallas import tpu as pltpu
from jax.sharding import PartitionSpec as P

MESH = pl.DeviceIdType.MESH
HIGHEST = lax.Precision.HIGHEST
DEPTH = 2
MASS = (1.0 / 36.0, 1.0 / 12.0, 1.0 / 45.0)
STIFF = (0.0, 1.0, 4.0 / 3.0)
DIRECTIONS = [(dr, dl) for dr in (-1, 1, 0) for dl in (-1, 1, 0) if (dr, dl) != (0, 0)]


def mode_weight(i, j, k):
    return (
        STIFF[i] * MASS[j] * MASS[k]
        + MASS[i] * STIFF[j] * MASS[k]
        + MASS[i] * MASS[j] * STIFF[k]
    )


def to_modes(a, b, c):
    double = b + b
    ends = a + c
    return ends + (double + double), a - c, ends - double


def from_modes(g0, g1, g2):
    ends = g0 + g2
    half = (g0 + g0) - g2
    return ends + g1, half + half, ends - g1


def kernel(
    n_steps, n_prev, n_layers, n_rad, n_lat, dof_count,
    residual, prev_basis, layer_ids, viscosity_in, shifts_in,
    new_basis, gram,
    viscosity, shifts,
    res_v, prev_v, ids_v, pick, pick_t, field, prev_d, wide, parts, pack, side, eta, eta_wide,
    rows, late, row_lat, row_rad,
    known, in_sem, send_sem, recv_sem, esend_sem, erecv_sem, gsend_sem, grecv_sem,
):
    rad = lax.axis_index("rad")
    lat = lax.axis_index("lat")
    n_exchange = n_steps // DEPTH
    up = 2 * DEPTH
    down = 2 * DEPTH - 1

    barrier = pltpu.get_barrier_semaphore()

    def here(dr, dl):
        inside = None
        for value, step, count in ((rad, dr, n_rad), (lat, dl, n_lat)):
            if step:
                test = value < count - 1 if step > 0 else value > 0
                inside = test if inside is None else jnp.logical_and(inside, test)
        return inside

    def around(axis, distance):
        if axis == 0:
            return {"lat": lax.rem(lat + distance + n_lat, n_lat), "rad": rad}
        return {"lat": lat, "rad": lax.rem(rad + distance + n_rad, n_rad)}

    corners = 0
    for axis in range(2):
        for d in (-1, 1):
            pl.semaphore_signal(barrier, inc=1, device_id=around(axis, d), device_id_type=MESH)
    for dr in (-1, 1):
        for dl in (-1, 1):
            corners = corners + jnp.where(here(dr, dl), 1, 0)

            @pl.when(here(dr, dl))
            def _():
                pl.semaphore_signal(
                    barrier, inc=1, device_id={"lat": lat + dl, "rad": rad + dr}, device_id_type=MESH
                )

    def tell(r):
        for axis, count in enumerate((n_lat, n_rad)):
            if 2**r % count:
                for d in (-(2**r), 2**r):
                    pl.semaphore_signal(
                        known.at[axis, r], inc=1, device_id=around(axis, d), device_id_type=MESH
                    )

    def hear(r):
        for axis, count in enumerate((n_lat, n_rad)):
            if 2**r % count:
                pl.semaphore_wait(known.at[axis, r], 2)

    copies = [
        pltpu.make_async_copy(residual, res_v, in_sem.at[0]),
        pltpu.make_async_copy(layer_ids, ids_v, in_sem.at[1]),
        pltpu.make_async_copy(viscosity_in, viscosity, in_sem.at[3]),
        pltpu.make_async_copy(shifts_in, shifts, in_sem.at[4]),
        pltpu.make_async_copy(prev_basis, prev_v, in_sem.at[2]),
    ]
    for copy in copies:
        copy.start()

    rows[...] = jnp.zeros(rows.shape, jnp.float32)
    late[...] = jnp.zeros(late.shape, jnp.float32)
    sub = lax.broadcasted_iota(jnp.int32, (8, 128), 0)
    lane = lax.broadcasted_iota(jnp.int32, (8, 128), 1)
    upper_rows = sub < 4

    row_id = lax.broadcasted_iota(jnp.int32, (256, 256), 0)
    col_id = lax.broadcasted_iota(jnp.int32, (256, 256), 1)
    pick[...] = (row_id == jnp.where(col_id < 128, 2 * col_id, 2 * col_id - 255)).astype(jnp.float32).astype(jnp.bfloat16)
    pick_t[...] = (col_id == jnp.where(row_id < 128, 2 * row_id, 2 * row_id - 255)).astype(jnp.float32).astype(jnp.bfloat16)

    def permute(values, table):
        top = values.astype(jnp.bfloat16)
        rest = values - top.astype(jnp.float32)
        middle = rest.astype(jnp.bfloat16)
        last = (rest - middle.astype(jnp.float32)).astype(jnp.bfloat16)
        moved = jnp.dot(
            jnp.concatenate([top, middle, last], axis=0), table[...], preferred_element_type=jnp.float32
        )
        n = values.shape[0]
        return (moved[:n] + moved[n : 2 * n]) + moved[2 * n :]

    def split_y(values, store):
        split = permute(values.reshape(64, 256), pick)
        store(0, split[:, :128].reshape(8, 8, 128))
        store(1, split[:, 128:].reshape(8, 8, 128))

    def split_residual(c):
        def store(y, value):
            field[0, c, 4:12, y] = value

        split_y(res_v[c], store)

    copies[1].wait()
    copies[2].wait()
    for a in range(4):
        ids = ids_v[a]
        values = jnp.zeros(ids.shape, jnp.float32)
        for layer in range(n_layers):
            values = jnp.where(ids == layer, viscosity[layer], values)
        eta[1, 2 + a] = jnp.concatenate([values, values], axis=0)

    def pack_sides(e, k, c):
        for p in range(8):
            even = field[k, c, 4 + p, 0]
            odd = field[k, c, 4 + p, 1]
            pack[e, c, 0, p] = jnp.where(upper_rows, even, pltpu.roll(odd, 4, 0))
            pack[e, c, 1, p] = jnp.where(upper_rows, pltpu.roll(even, 4, 0), odd)

    def halo_copy(e, c, n):
        dr, dl = DIRECTIONS[n]
        k = e * DEPTH
        source, target, size = {
            1: (8 - up, 4 - up, up), -1: (0, 12, down), 0: (0, 4, 8)
        }[dr]
        if dl == 0:
            src = field.at[k, c, pl.ds(4 + source, size)]
            dst = field.at[k, c, pl.ds(target, size)]
        else:
            src = pack.at[e, c, 0 if dl < 0 else 1, pl.ds(source, size)]
            dst = side.at[e, c, 1 if dl < 0 else 0, pl.ds(target, size)]
        return pltpu.make_async_remote_copy(
            src_ref=src, dst_ref=dst, send_sem=send_sem.at[e, c, n], recv_sem=recv_sem.at[e, c, n],
            device_id={"lat": lat + dl, "rad": rad + dr}, device_id_type=MESH,
        )

    def eta_copy(n):
        dr, dl = DIRECTIONS[n]
        source, target, size = {1: (2, 0, 2), -1: (0, 6, 2), 0: (0, 2, 4)}[dr]
        return pltpu.make_async_remote_copy(
            src_ref=eta.at[1, pl.ds(2 + source, size)],
            dst_ref=eta.at[1 - dl, pl.ds(target, size)],
            send_sem=esend_sem.at[n], recv_sem=erecv_sem.at[n],
            device_id={"lat": lat + dl, "rad": rad + dr}, device_id_type=MESH,
        )

    def each_direction(receive, act):
        for n, (dr, dl) in enumerate(DIRECTIONS):
            test = here(-dr, -dl) if receive else here(dr, dl)

            @pl.when(test)
            def _():
                act(n)

    def put_wide(p, c, tile, values):
        for slot, value in enumerate(values):
            wide[c, p, slot, tile * 8 : tile * 8 + 8] = value
            if tile == 0:
                wide[c, p, slot, 16:24] = value

    def widen(p, c, tile, even, odd):
        put_wide(p, c, tile, (even, odd, jnp.where(lane < 127, pltpu.roll(even, 127, 1), 0.0)))

    def widen_own(k, c, planes):
        for p in planes:
            widen(p, c, 0, field[k, c, p, 0], field[k, c, p, 1])

    def widen_sides(e, c, planes):
        for p in planes:
            below = side[e, c, 0, p]
            above = side[e, c, 1, p]
            widen(
                p, c, 1,
                jnp.where(upper_rows, above, pltpu.roll(below, 4, 0)),
                jnp.where(upper_rows, pltpu.roll(above, 4, 0), below),
            )

    width = n_prev + n_steps + 1

    def dot_sums(n, c, sums):
        def tile(m, p, y):
            return prev_d[m, c, p, y] if m < n_prev else field[m - n_prev, c, 4 + p, y]

        def body(half, sums):
            sums = list(sums)
            for q in range(4):
                for y in range(2):
                    new = tile(n, half * 4 + q, y)
                    for m in range(n + 1):
                        other = new if m == n else tile(m, half * 4 + q, y)
                        sums[m] = sums[m] + new * other
            return tuple(sums)

        return lax.fori_loop(0, 2, body, sums)

    def put_rows(n, sums):
        for m in range(n + 1):
            total = jnp.sum(sums[m], axis=0, keepdims=True)
            rows[n * width + m : n * width + m + 1] = total
            if m != n:
                rows[m * width + n : m * width + n + 1] = total

    def dots(n):
        zero = jnp.zeros((8, 128), jnp.float32)
        put_rows(n, lax.fori_loop(0, 3, lambda c, sums: dot_sums(n, c, sums), (zero,) * (n + 1)))

    def planes_modes(p, c):
        nodes = [
            [wide[c, p, slot, pl.ds(start, 8, stride=2)] for start in range(3)] for slot in range(3)
        ]
        lines = [to_modes(*nodes[slot]) for slot in range(3)]
        return [to_modes(lines[0][i], lines[1][i], lines[2][i]) for i in range(3)]

    def put_plane(p, c, modes):
        lines = [from_modes(*modes[i]) for i in range(3)]
        for slot in range(3):
            low, mid, high = from_modes(lines[0][slot], lines[1][slot], lines[2][slot])
            parts[c, p, slot, pl.ds(0, 8, stride=2)] = low + pltpu.roll(high, 1, 0)
            parts[c, p, slot, pl.ds(1, 8, stride=2)] = mid

    def apply(c, first, last, low_plane, high_plane):
        below = planes_modes(2 * first, c)
        carried = None
        for a in range(first, last):
            visc = eta_wide[a]
            weight = {}
            for i in range(3):
                for j in range(i, 3):
                    for l in range(j, 3):
                        if l > 0:
                            weight[i, j, l] = visc * mode_weight(i, j, l)
            middle = planes_modes(2 * a + 1, c)
            above = planes_modes(2 * a + 2, c)
            at_low = [[None] * 3 for _ in range(3)]
            at_mid = [[None] * 3 for _ in range(3)]
            at_high = [[None] * 3 for _ in range(3)]
            for i in range(3):
                for j in range(3):
                    m = to_modes(below[i][j], middle[i][j], above[i][j])
                    g = [
                        None if i + j + l == 0 else m[l] * weight[tuple(sorted((i, j, l)))]
                        for l in range(3)
                    ]
                    if g[0] is None:
                        twice = g[2] + g[2]
                        out = (g[2] + g[1], -twice, g[2] - g[1])
                    else:
                        out = from_modes(*g)
                    at_low[i][j] = out[0] if carried is None else out[0] + carried[i][j]
                    at_mid[i][j] = out[1]
                    at_high[i][j] = out[2]
            if low_plane <= 2 * a <= high_plane:
                put_plane(2 * a, c, at_low)
            if low_plane <= 2 * a + 1 <= high_plane:
                put_plane(2 * a + 1, c, at_mid)
            carried = at_high
            below = above

    keep_rad = jnp.where(rad == n_rad - 1, 0.0, 1.0)
    keep_lat = jnp.where(jnp.logical_and(upper_rows, lat == n_lat - 1), 0.0, 1.0)

    def advance(k, c, planes, tiles, outer):
        shift = shifts[k]
        for p in planes:
            for tile in tiles:
                at = slice(tile * 8, tile * 8 + 8)
                low = parts[c, p, 0, at]
                high = parts[c, p, 2, at]
                even = low + jnp.where(lane > 0, pltpu.roll(high, 1, 1), 0.0) - shift * wide[c, p, 0, at]
                odd = parts[c, p, 1, at] - shift * wide[c, p, 1, at]
                values = [even, odd]
                if outer:
                    after = jnp.where(lane < 127, pltpu.roll(low, 127, 1) + high, 0.0)
                    values.append(after - shift * wide[c, p, 2, at])
                if p >= 12:
                    values = [value * keep_rad for value in values]
                if tile == 1:
                    values = [value * keep_lat for value in values]
                if tile == 0 and 4 <= p < 12:
                    field[k + 1, c, p, 0] = values[0]
                    field[k + 1, c, p, 1] = values[1]
                if outer:
                    put_wide(p, c, tile, values)

    def put_out(k):
        lines = []
        for c in range(3):
            even = field[k + 1, c, 4:12, 0].reshape(64, 128)
            odd = field[k + 1, c, 4:12, 1].reshape(64, 128)
            lines.append(jnp.concatenate([even, odd], axis=1))
        merged = permute(jnp.concatenate(lines, axis=0), pick_t)
        new_basis[k] = merged.reshape(3, 8, 8, 256)

    def zero_edges():
        def clear(ref):
            ref[...] = jnp.zeros(ref.shape, jnp.float32)

        @pl.when(rad == 0)
        def _():
            for e in range(n_exchange):
                clear(field.at[e * DEPTH, :, 4 - up : 4])
                clear(side.at[e, :, :, 4 - up : 4])
            clear(eta.at[:, 0:2])

        @pl.when(rad == n_rad - 1)
        def _():
            for e in range(n_exchange):
                clear(field.at[e * DEPTH, :, 12 : 12 + down])
                clear(side.at[e, :, :, 12 : 12 + down])
            clear(eta.at[:, 6:8])

        @pl.when(lat == 0)
        def _():
            for e in range(n_exchange):
                clear(side.at[e, :, 0])
            clear(eta.at[0])

        @pl.when(lat == n_lat - 1)
        def _():
            for e in range(n_exchange):
                clear(side.at[e, :, 1])
            clear(eta.at[2])

    def send_halo(e, c):
        each_direction(False, lambda n: halo_copy(e, c, n).start())

    copies[0].wait()
    split_residual(0)
    pack_sides(0, 0, 0)
    pl.semaphore_wait(barrier, 4 + corners)
    each_direction(False, lambda n: eta_copy(n).start())
    send_halo(0, 0)
    for c in range(1, 3):
        split_residual(c)
        pack_sides(0, 0, c)
        send_halo(0, c)
    tell(0)

    zero_edges()
    for c in range(3):
        widen_own(0, c, range(4, 12))
    copies[4].wait()
    copies[3].wait()
    for m in range(n_prev):
        for c in range(3):

            def store_prev(y, value):
                prev_d[m, c, :, y] = value

            split_y(prev_v[m, c], store_prev)
    for m in range(n_prev + 1):
        dots(m)
    hear(0)
    tell(1)
    each_direction(True, lambda n: eta_copy(n).wait_recv())
    for a in range(8):
        eta_wide[a] = jnp.where(upper_rows, eta[1, a], jnp.where(sub < 6, eta[2, a], eta[0, a]))

    low, high = 4 - up, 12 + down
    for e in range(n_exchange):
        k = e * DEPTH
        final = e == n_exchange - 1

        def component(c, nothing):
            each_direction(True, lambda n: halo_copy(e, c, n).wait_recv())
            widen_own(k, c, list(range(low, 4)) + list(range(12, high)))
            widen_sides(e, c, range(low, high))
            for step in range(DEPTH):
                left = DEPTH - 1 - step
                apply(c, 1 - left, 6 + left, 4 - 2 * left, 11 + left)
                last = step == DEPTH - 1
                advance(
                    k + step, c, range(4 - 2 * left, 12 + left), (0,) if last else (0, 1),
                    not (last and final),
                )
            if final:
                for j in range(k + 1, n_steps + 1):
                    n = n_prev + j
                    sums = tuple(late[j - k - 1, m] for m in range(n + 1))
                    for m, value in enumerate(dot_sums(n, c, sums)):
                        late[j - k - 1, m] = value
            else:
                pack_sides(e + 1, k + DEPTH, c)
                send_halo(e + 1, c)
            return nothing

        lax.fori_loop(0, 3, component, 0)
        if not final:
            hear(1)
            tell(2)
            for j in range(k + 1, k + DEPTH + 1):
                dots(n_prev + j)
                put_out(j - 1)

    hear(2)
    for j in range(n_steps - DEPTH + 1, n_steps + 1):
        n = n_prev + j
        put_rows(n, [late[j - (n_steps - DEPTH) - 1, m] for m in range(n + 1)])
    ones = jnp.ones((8, 128), jnp.float32)
    local = lax.dot_general(
        ones, rows[...], (((1,), (1,)), ((), ())), precision=HIGHEST, preferred_element_type=jnp.float32
    )
    row_lat[lat] = local[0:1]

    def row_copy(stage, d):
        buffer, me, count = (row_lat, lat, n_lat) if stage == 0 else (row_rad, rad, n_rad)
        peer = lax.rem(me + d, count)
        target = {"lat": peer, "rad": rad} if stage == 0 else {"lat": lat, "rad": peer}
        return pltpu.make_async_remote_copy(
            src_ref=buffer.at[me], dst_ref=buffer.at[me],
            send_sem=gsend_sem.at[stage, d], recv_sem=grecv_sem.at[stage, d],
            device_id=target, device_id_type=MESH,
        )

    for d in range(1, n_lat):
        row_copy(0, d).start()
    for j in range(n_steps - DEPTH + 1, n_steps + 1):
        put_out(j - 1)
    for d in range(1, n_lat):
        row_copy(0, d).wait_recv()
    total = row_lat[0]
    for d in range(1, n_lat):
        total = total + row_lat[d]
    row_rad[rad] = total
    for d in range(1, n_rad):
        row_copy(1, d).start()
    each_direction(False, lambda n: eta_copy(n).wait_send())
    for e in range(n_exchange):
        for c in range(3):
            each_direction(False, lambda n: halo_copy(e, c, n).wait_send())
    for d in range(1, n_lat):
        row_copy(0, d).wait_send()
    for d in range(1, n_rad):
        row_copy(1, d).wait_recv()
    total = row_rad[0]
    for d in range(1, n_rad):
        total = total + row_rad[d]
    total = total * (1.0 / dof_count)
    for i in range(width):
        line = total if i == 0 else pltpu.roll(jnp.broadcast_to(total, (8, 128)), 128 - i * width, 1)[0:1]
        gram[i : i + 1, :] = line[:, :width]
    for d in range(1, n_rad):
        row_copy(1, d).wait_send()


def solution(mesh):
    n_lat = mesh.shape["lat"]
    n_rad = mesh.shape["rad"]

    def on_device(residual, prev_basis, layer_ids, viscosity, shifts):
        n_steps = shifts.shape[0]
        n_prev = prev_basis.shape[0]
        width = n_prev + n_steps + 1
        n_exchange = n_steps // DEPTH
        dof_count = residual.size * n_lat * n_rad
        f32 = jnp.float32
        dma = pltpu.SemaphoreType.DMA
        return pl.pallas_call(
            functools.partial(
                kernel, n_steps, n_prev, viscosity.shape[0], n_rad, n_lat, dof_count
            ),
            out_shape=(
                jax.ShapeDtypeStruct((n_steps,) + residual.shape, f32),
                jax.ShapeDtypeStruct((width, width), f32),
            ),
            in_specs=[pl.BlockSpec(memory_space=pltpu.HBM)] * 5,
            out_specs=(
                pl.BlockSpec(memory_space=pltpu.VMEM),
                pl.BlockSpec(memory_space=pltpu.VMEM),
            ),
            scratch_shapes=[
                pltpu.SMEM(viscosity.shape, f32),
                pltpu.SMEM(shifts.shape, f32),
                pltpu.VMEM(residual.shape, f32),
                pltpu.VMEM(prev_basis.shape, f32),
                pltpu.VMEM(layer_ids.shape, jnp.int32),
                pltpu.VMEM((256, 256), jnp.bfloat16),
                pltpu.VMEM((256, 256), jnp.bfloat16),
                pltpu.VMEM((n_steps + 1, 3, 16, 2, 8, 128), f32),
                pltpu.VMEM((n_prev, 3, 8, 2, 8, 128), f32),
                pltpu.VMEM((3, 16, 3, 24, 128), f32),
                pltpu.VMEM((3, 16, 3, 16, 128), f32),
                pltpu.VMEM((n_exchange, 3, 2, 8, 8, 128), f32),
                pltpu.VMEM((n_exchange, 3, 2, 16, 8, 128), f32),
                pltpu.VMEM((3, 8, 8, 128), f32),
                pltpu.VMEM((8, 8, 128), f32),
                pltpu.VMEM((128, 128), f32),
                pltpu.VMEM((DEPTH, width, 8, 128), f32),
                pltpu.VMEM((n_lat, 1, 128), f32),
                pltpu.VMEM((n_rad, 1, 128), f32),
                pltpu.SemaphoreType.REGULAR((2, 3)),
                dma((5,)),
                dma((n_exchange, 3, 8)),
                dma((n_exchange, 3, 8)),
                dma((8,)),
                dma((8,)),
                dma((2, max(n_lat, n_rad))),
                dma((2, max(n_lat, n_rad))),
            ],
            compiler_params=pltpu.CompilerParams(collective_id=0, has_side_effects=True, vmem_limit_bytes=24 * 2**20),
        )(*(pltpu.with_memory_space_constraint(x, pltpu.HBM) for x in (residual, prev_basis, layer_ids, viscosity, shifts)))

    placed = (P(None, "rad", "lat", None), P(None, None, "rad", "lat", None), P("rad", "lat", None), P(), P())
    return jax.shard_map(
        on_device,
        mesh=mesh,
        in_specs=placed,
        out_specs=(P(None, None, "rad", "lat", None), P()),
        check_vma=False,
    )
```

time: 41.9 us -> 35.5 us (0.85)
  Pallas kernels: 38.5 us -> 33.2 us
  local copies, waits for them, and re-layouts: 2.67 us -> 1.48 us
    pallas_call x1, Pallas kernels: 38.5 us -> 33.2 us  [on_device(): pl.pallas_call(functools.partial(kernel, n_steps, n_prev, viscosity.shape...]
    unnamed x4 -> x2, local copies, waits for them, and re-layouts: 2.67 us -> 1.48 us
where the time goes in v1:
time: 35.5 us; the launch traced here: 35.4 us
  Pallas kernels  33.2 us (94%)
  local copies, waits for them, and re-layouts  1.48 us (4%)
  between operations  0.64 us (2%)
    pallas_call x1, Pallas kernels, on_device(): pl.pallas_call(functools.partial(kernel, n_steps, n_prev, viscosity.shape...  33.2 us
    unnamed x2, local copies, waits for them, and re-layouts  1.48 us

profile of v1, /device:TPU:1, one launch (start us, length us, event | category | flops | bytes accessed | tf_op | source)
XLA Modules:
  0.0 35.4 jit_solution(18286994657990313922)
XLA Ops:
  0.6 33.2 %shard_map.68 = (f32[4,3,8,8,256]{4,3,2,1,0:T(8,128)S(1)}, f32[9,9]{1,0:T(8,128)S(1)}) custom-call(f32[3,8,8,256]{3,2,1,0:T(8,128)} %residual.1, f32[4,3,8,8,256]{4,3,2,1,0:T(8,128)} %prev_basis.1, s32[4,4,128]{2,1,0:T(4,128)} %layer_ids.1, f32[8]{0:T(128)} %viscosity_in.1, f32[4]{0:T(128)} %shifts_in.1), custom_call_target="tpu_custom_call" | custom-call | tf_op jit(solution)/shard_map/pallas_call | solution.py:492
  33.9 0.9 %copy.9 = f32[4,3,8,8,256]{4,3,2,1,0:T(8,128)} copy(f32[4,3,8,8,256]{4,3,2,1,0:T(8,128)S(1)} %get-tuple-element.4) | data formatting | bytes 1572864
  34.8 0.6 %copy.10 = f32[9,9]{1,0:T(8,128)} copy(f32[9,9]{1,0:T(8,128)S(1)} %get-tuple-element.5) | data formatting | bytes 648

commit v2 on v1

--- a/solution.py
+++ b/solution.py
@@ -12,7 +12,7 @@
 DEPTH = 2
 MASS = (1.0 / 36.0, 1.0 / 12.0, 1.0 / 45.0)
 STIFF = (0.0, 1.0, 4.0 / 3.0)
-DIRECTIONS = [(dr, dl) for dr in (-1, 1, 0) for dl in (-1, 1, 0) if (dr, dl) != (0, 0)]
+DIRECTIONS = [(-1, 0), (1, 0), (-1, -1), (-1, 1), (1, -1), (1, 1), (0, -1), (0, 1)]
 
 
 def mode_weight(i, j, k):
@@ -24,15 +24,16 @@
 
 
 def to_modes(a, b, c):
-    double = b + b
     ends = a + c
-    return ends + (double + double), a - c, ends - double
+    return ends + (b + b), a - c, ends - b
 
 
 def from_modes(g0, g1, g2):
     ends = g0 + g2
-    half = (g0 + g0) - g2
-    return ends + g1, half + half, ends - g1
+    return ends + g1, (g0 + g0) - g2, ends - g1
+
+
+WEIGHTS = [(i, j, l) for i in range(3) for j in range(i, 3) for l in range(j, 3) if l > 0]
 
 
 def kernel(
@@ -50,48 +51,6 @@
     up = 2 * DEPTH
     down = 2 * DEPTH - 1
 
-    barrier = pltpu.get_barrier_semaphore()
-
-    def here(dr, dl):
-        inside = None
-        for value, step, count in ((rad, dr, n_rad), (lat, dl, n_lat)):
-            if step:
-                test = value < count - 1 if step > 0 else value > 0
-                inside = test if inside is None else jnp.logical_and(inside, test)
-        return inside
-
-    def around(axis, distance):
-        if axis == 0:
-            return {"lat": lax.rem(lat + distance + n_lat, n_lat), "rad": rad}
-        return {"lat": lat, "rad": lax.rem(rad + distance + n_rad, n_rad)}
-
-    corners = 0
-    for axis in range(2):
-        for d in (-1, 1):
-            pl.semaphore_signal(barrier, inc=1, device_id=around(axis, d), device_id_type=MESH)
-    for dr in (-1, 1):
-        for dl in (-1, 1):
-            corners = corners + jnp.where(here(dr, dl), 1, 0)
-
-            @pl.when(here(dr, dl))
-            def _():
-                pl.semaphore_signal(
-                    barrier, inc=1, device_id={"lat": lat + dl, "rad": rad + dr}, device_id_type=MESH
-                )
-
-    def tell(r):
-        for axis, count in enumerate((n_lat, n_rad)):
-            if 2**r % count:
-                for d in (-(2**r), 2**r):
-                    pl.semaphore_signal(
-                        known.at[axis, r], inc=1, device_id=around(axis, d), device_id_type=MESH
-                    )
-
-    def hear(r):
-        for axis, count in enumerate((n_lat, n_rad)):
-            if 2**r % count:
-                pl.semaphore_wait(known.at[axis, r], 2)
-
     copies = [
         pltpu.make_async_copy(residual, res_v, in_sem.at[0]),
         pltpu.make_async_copy(layer_ids, ids_v, in_sem.at[1]),
@@ -102,11 +61,56 @@
     for copy in copies:
         copy.start()
 
+    barrier = pltpu.get_barrier_semaphore()
+
+    def here(dr, dl):
+        inside = None
+        for value, step, count in ((rad, dr, n_rad), (lat, dl, n_lat)):
+            if step:
+                test = value < count - 1 if step > 0 else value > 0
+                inside = test if inside is None else jnp.logical_and(inside, test)
+        return inside
+
+    def around(axis, distance):
+        if axis == 0:
+            return {"lat": lax.rem(lat + distance + n_lat, n_lat), "rad": rad}
+        return {"lat": lat, "rad": lax.rem(rad + distance + n_rad, n_rad)}
+
+    corners = 0
+    for axis in range(2):
+        for d in (-1, 1):
+            pl.semaphore_signal(barrier, inc=1, device_id=around(axis, d), device_id_type=MESH)
+    for dr in (-1, 1):
+        for dl in (-1, 1):
+            corners = corners + jnp.where(here(dr, dl), 1, 0)
+
+            @pl.when(here(dr, dl))
+            def _():
+                pl.semaphore_signal(
+                    barrier, inc=1, device_id={"lat": lat + dl, "rad": rad + dr}, device_id_type=MESH
+                )
+
+    def tell(r):
+        for axis, count in enumerate((n_lat, n_rad)):
+            if 2**r % count:
+                for d in (-(2**r), 2**r):
+                    pl.semaphore_signal(
+                        known.at[axis, r], inc=1, device_id=around(axis, d), device_id_type=MESH
+                    )
+
+    def hear(r):
+        for axis, count in enumerate((n_lat, n_rad)):
+            if 2**r % count:
+                pl.semaphore_wait(known.at[axis, r], 2)
+
     rows[...] = jnp.zeros(rows.shape, jnp.float32)
     late[...] = jnp.zeros(late.shape, jnp.float32)
     sub = lax.broadcasted_iota(jnp.int32, (8, 128), 0)
     lane = lax.broadcasted_iota(jnp.int32, (8, 128), 1)
     upper_rows = sub < 4
+    double = [jnp.where(sub % 2 == 0, 1.0, 2.0) * 2.0**q for q in range(3)]
+    half = [jnp.where(sub % 2 == 0, 1.0, 0.5) * 0.5**q for q in range(3)]
+    square = [jnp.where(sub % 2 == 0, 1.0, 4.0) * 4.0**q for q in range(3)]
 
     row_id = lax.broadcasted_iota(jnp.int32, (256, 256), 0)
     col_id = lax.broadcasted_iota(jnp.int32, (256, 256), 1)
@@ -137,12 +141,16 @@
 
     copies[1].wait()
     copies[2].wait()
+    layers = []
     for a in range(4):
         ids = ids_v[a]
         values = jnp.zeros(ids.shape, jnp.float32)
         for layer in range(n_layers):
             values = jnp.where(ids == layer, viscosity[layer], values)
-        eta[1, 2 + a] = jnp.concatenate([values, values], axis=0)
+        layers.append(values)
+
+    for h in range(2):
+        eta[1, 1 + h] = jnp.concatenate(layers[2 * h : 2 * h + 2], axis=0)
 
     def pack_sides(e, k, c):
         for p in range(8):
@@ -170,16 +178,18 @@
 
     def eta_copy(n):
         dr, dl = DIRECTIONS[n]
-        source, target, size = {1: (2, 0, 2), -1: (0, 6, 2), 0: (0, 2, 4)}[dr]
+        source, target, size = {1: (1, 0, 1), -1: (0, 3, 1), 0: (0, 1, 2)}[dr]
         return pltpu.make_async_remote_copy(
-            src_ref=eta.at[1, pl.ds(2 + source, size)],
+            src_ref=eta.at[1, pl.ds(1 + source, size)],
             dst_ref=eta.at[1 - dl, pl.ds(target, size)],
             send_sem=esend_sem.at[n], recv_sem=erecv_sem.at[n],
             device_id={"lat": lat + dl, "rad": rad + dr}, device_id_type=MESH,
         )
 
-    def each_direction(receive, act):
+    def each_direction(receive, act, which=range(8)):
         for n, (dr, dl) in enumerate(DIRECTIONS):
+            if n not in which:
+                continue
             test = here(-dr, -dl) if receive else here(dr, dl)
 
             @pl.when(test)
@@ -193,6 +203,8 @@
                 wide[c, p, slot, 16:24] = value
 
     def widen(p, c, tile, even, odd):
+        even = even * double[p % 2]
+        odd = odd * double[p % 2 + 1]
         put_wide(p, c, tile, (even, odd, jnp.where(lane < 127, pltpu.roll(even, 127, 1), 0.0)))
 
     def widen_own(k, c, planes):
@@ -256,13 +268,6 @@
         below = planes_modes(2 * first, c)
         carried = None
         for a in range(first, last):
-            visc = eta_wide[a]
-            weight = {}
-            for i in range(3):
-                for j in range(i, 3):
-                    for l in range(j, 3):
-                        if l > 0:
-                            weight[i, j, l] = visc * mode_weight(i, j, l)
             middle = planes_modes(2 * a + 1, c)
             above = planes_modes(2 * a + 2, c)
             at_low = [[None] * 3 for _ in range(3)]
@@ -272,12 +277,11 @@
                 for j in range(3):
                     m = to_modes(below[i][j], middle[i][j], above[i][j])
                     g = [
-                        None if i + j + l == 0 else m[l] * weight[tuple(sorted((i, j, l)))]
+                        None if i + j + l == 0 else m[l] * eta_wide[a, WEIGHTS.index(tuple(sorted((i, j, l))))]
                         for l in range(3)
                     ]
                     if g[0] is None:
-                        twice = g[2] + g[2]
-                        out = (g[2] + g[1], -twice, g[2] - g[1])
+                        out = (g[2] + g[1], -g[2], g[2] - g[1])
                     else:
                         out = from_modes(*g)
                     at_low[i][j] = out[0] if carried is None else out[0] + carried[i][j]
@@ -300,19 +304,20 @@
                 at = slice(tile * 8, tile * 8 + 8)
                 low = parts[c, p, 0, at]
                 high = parts[c, p, 2, at]
-                even = low + jnp.where(lane > 0, pltpu.roll(high, 1, 1), 0.0) - shift * wide[c, p, 0, at]
-                odd = parts[c, p, 1, at] - shift * wide[c, p, 1, at]
+                moved = jnp.where(lane > 0, pltpu.roll(high, 1, 1), 0.0)
+                even = square[p % 2] * (low + moved) - shift * wide[c, p, 0, at]
+                odd = square[p % 2 + 1] * parts[c, p, 1, at] - shift * wide[c, p, 1, at]
                 values = [even, odd]
                 if outer:
                     after = jnp.where(lane < 127, pltpu.roll(low, 127, 1) + high, 0.0)
-                    values.append(after - shift * wide[c, p, 2, at])
+                    values.append(square[p % 2] * after - shift * wide[c, p, 2, at])
                 if p >= 12:
                     values = [value * keep_rad for value in values]
                 if tile == 1:
                     values = [value * keep_lat for value in values]
                 if tile == 0 and 4 <= p < 12:
-                    field[k + 1, c, p, 0] = values[0]
-                    field[k + 1, c, p, 1] = values[1]
+                    field[k + 1, c, p, 0] = values[0] * half[p % 2]
+                    field[k + 1, c, p, 1] = values[1] * half[p % 2 + 1]
                 if outer:
                     put_wide(p, c, tile, values)
 
@@ -334,14 +339,14 @@
             for e in range(n_exchange):
                 clear(field.at[e * DEPTH, :, 4 - up : 4])
                 clear(side.at[e, :, :, 4 - up : 4])
-            clear(eta.at[:, 0:2])
+            clear(eta.at[:, 0:1])
 
         @pl.when(rad == n_rad - 1)
         def _():
             for e in range(n_exchange):
                 clear(field.at[e * DEPTH, :, 12 : 12 + down])
                 clear(side.at[e, :, :, 12 : 12 + down])
-            clear(eta.at[:, 6:8])
+            clear(eta.at[:, 3:4])
 
         @pl.when(lat == 0)
         def _():
@@ -355,8 +360,8 @@
                 clear(side.at[e, :, 1])
             clear(eta.at[2])
 
-    def send_halo(e, c):
-        each_direction(False, lambda n: halo_copy(e, c, n).start())
+    def send_halo(e, c, which=range(8)):
+        each_direction(False, lambda n: halo_copy(e, c, n).start(), which)
 
     copies[0].wait()
     split_residual(0)
@@ -387,8 +392,15 @@
     hear(0)
     tell(1)
     each_direction(True, lambda n: eta_copy(n).wait_recv())
-    for a in range(8):
-        eta_wide[a] = jnp.where(upper_rows, eta[1, a], jnp.where(sub < 6, eta[2, a], eta[0, a]))
+    for h in range(4):
+        own = eta[1, h]
+        beside = jnp.where(sub % 4 < 2, eta[2, h], eta[0, h])
+        for half_row, visc in enumerate((
+            jnp.where(upper_rows, own, pltpu.roll(beside, 4, 0)),
+            jnp.where(upper_rows, pltpu.roll(own, 4, 0), beside),
+        )):
+            for q, modes in enumerate(WEIGHTS):
+                eta_wide[2 * h + half_row, q] = visc * mode_weight(*modes)
 
     low, high = 4 - up, 12 + down
     for e in range(n_exchange):
@@ -414,8 +426,9 @@
                     for m, value in enumerate(dot_sums(n, c, sums)):
                         late[j - k - 1, m] = value
             else:
+                send_halo(e + 1, c, range(2))
                 pack_sides(e + 1, k + DEPTH, c)
-                send_halo(e + 1, c)
+                send_halo(e + 1, c, range(2, 8))
             return nothing
 
         lax.fori_loop(0, 3, component, 0)
@@ -477,6 +490,17 @@
         row_copy(1, d).wait_send()
 
 
+def leave(vectors, sums, new_basis, gram, sems):
+    copies = [
+        pltpu.make_async_copy(vectors, new_basis, sems.at[0]),
+        pltpu.make_async_copy(sums, gram, sems.at[1]),
+    ]
+    for copy in copies:
+        copy.start()
+    for copy in copies:
+        copy.wait()
+
+
 def solution(mesh):
     n_lat = mesh.shape["lat"]
     n_rad = mesh.shape["rad"]
@@ -489,7 +513,7 @@
         dof_count = residual.size * n_lat * n_rad
         f32 = jnp.float32
         dma = pltpu.SemaphoreType.DMA
-        return pl.pallas_call(
+        vectors, sums = pl.pallas_call(
             functools.partial(
                 kernel, n_steps, n_prev, viscosity.shape[0], n_rad, n_lat, dof_count
             ),
@@ -516,8 +540,8 @@
                 pltpu.VMEM((3, 16, 3, 16, 128), f32),
                 pltpu.VMEM((n_exchange, 3, 2, 8, 8, 128), f32),
                 pltpu.VMEM((n_exchange, 3, 2, 16, 8, 128), f32),
-                pltpu.VMEM((3, 8, 8, 128), f32),
-                pltpu.VMEM((8, 8, 128), f32),
+                pltpu.VMEM((3, 4, 8, 128), f32),
+                pltpu.VMEM((8, len(WEIGHTS), 8, 128), f32),
                 pltpu.VMEM((128, 128), f32),
                 pltpu.VMEM((DEPTH, width, 8, 128), f32),
                 pltpu.VMEM((n_lat, 1, 128), f32),
@@ -534,6 +558,18 @@
             compiler_params=pltpu.CompilerParams(collective_id=0, has_side_effects=True, vmem_limit_bytes=24 * 2**20),
         )(*(pltpu.with_memory_space_constraint(x, pltpu.HBM) for x in (residual, prev_basis, layer_ids, viscosity, shifts)))
 
+        return pl.pallas_call(
+            leave,
+            out_shape=(
+                jax.ShapeDtypeStruct(vectors.shape, f32),
+                jax.ShapeDtypeStruct(sums.shape, f32),
+            ),
+            in_specs=[pl.BlockSpec(memory_space=pltpu.VMEM)] * 2,
+            out_specs=(pl.BlockSpec(memory_space=pltpu.HBM), pl.BlockSpec(memory_space=pltpu.HBM)),
+            scratch_shapes=[dma((2,))],
+            compiler_params=pltpu.CompilerParams(vmem_limit_bytes=2**20),
+        )(vectors, sums)
+
     placed = (P(None, "rad", "lat", None), P(None, None, "rad", "lat", None), P("rad", "lat", None), P(), P())
     return jax.shard_map(
         on_device,

time: 35.5 us -> 34.2 us (0.963)
  local copies, waits for them, and re-layouts: 1.48 us -> 0 us
    unnamed x2 -> x0, local copies, waits for them, and re-layouts: 1.48 us -> none
    pallas_call x0 -> x1, Pallas kernels: none -> 0.9 us  [on_device(): pl.pallas_call(leave, out_shape=(jax.ShapeDtypeStruct(vectors.shape, f32)...]
    pallas_call x1, Pallas kernels: 33.2 us -> 32.6 us  [on_device(): pl.pallas_call(functools.partial(kernel, n_steps, n_prev, viscosity.shape...]
where the time goes in v2:
time: 34.2 us; the launch traced here: 34.1 us
  Pallas kernels  33.5 us (98%)
  between operations  0.64 us (2%)
    pallas_call x1, Pallas kernels, on_device(): pl.pallas_call(functools.partial(kernel, n_steps, n_prev, viscosity.shape...  32.6 us
    pallas_call x1, Pallas kernels, on_device(): pl.pallas_call(leave, out_shape=(jax.ShapeDtypeStruct(vectors.shape, f32)...  0.9 us

profile of v2, /device:TPU:1, one launch (start us, length us, event | category | flops | bytes accessed | tf_op | source)
XLA Modules:
  0.0 34.1 jit_solution(15790969934594502048)
XLA Ops:
  0.6 32.6 %shard_map.68 = (f32[4,3,8,8,256]{4,3,2,1,0:T(8,128)S(1)}, f32[9,9]{1,0:T(8,128)S(1)}) custom-call(f32[3,8,8,256]{3,2,1,0:T(8,128)} %residual.1, f32[4,3,8,8,256]{4,3,2,1,0:T(8,128)} %prev_basis.1, s32[4,4,128]{2,1,0:T(4,128)} %layer_ids.1, f32[8]{0:T(128)} %viscosity_in.1, f32[4]{0:T(128)} %shifts_in.1), custom_call_target="tpu_custom_call" | custom-call | tf_op jit(solution)/shard_map/pallas_call | solution.py:516
  33.2 0.9 %shard_map.69 = (f32[4,3,8,8,256]{4,3,2,1,0:T(8,128)}, f32[9,9]{1,0:T(8,128)}) custom-call(f32[4,3,8,8,256]{4,3,2,1,0:T(8,128)S(1)} %get-tuple-element.4.vectors, f32[9,9]{1,0:T(8,128)S(1)} %get-tuple-element.5.sums), custom_call_target="tpu_custom_call" | custom-call | tf_op jit(solution)/shard_map/pallas_call | solution.py:561

commit v3 on v2

--- a/solution.py
+++ b/solution.py
@@ -37,7 +37,7 @@
 
 
 def kernel(
-    n_steps, n_prev, n_layers, n_rad, n_lat, dof_count,
+    n_steps, n_prev, n_layers, n_rad, n_lat,
     residual, prev_basis, layer_ids, viscosity_in, shifts_in,
     new_basis, gram,
     viscosity, shifts,
@@ -103,8 +103,6 @@
             if 2**r % count:
                 pl.semaphore_wait(known.at[axis, r], 2)
 
-    rows[...] = jnp.zeros(rows.shape, jnp.float32)
-    late[...] = jnp.zeros(late.shape, jnp.float32)
     sub = lax.broadcasted_iota(jnp.int32, (8, 128), 0)
     lane = lax.broadcasted_iota(jnp.int32, (8, 128), 1)
     upper_rows = sub < 4
@@ -115,7 +113,6 @@
     row_id = lax.broadcasted_iota(jnp.int32, (256, 256), 0)
     col_id = lax.broadcasted_iota(jnp.int32, (256, 256), 1)
     pick[...] = (row_id == jnp.where(col_id < 128, 2 * col_id, 2 * col_id - 255)).astype(jnp.float32).astype(jnp.bfloat16)
-    pick_t[...] = (col_id == jnp.where(row_id < 128, 2 * row_id, 2 * row_id - 255)).astype(jnp.float32).astype(jnp.bfloat16)
 
     def permute(values, table):
         top = values.astype(jnp.bfloat16)
@@ -376,6 +373,9 @@
     tell(0)
 
     zero_edges()
+    rows[...] = jnp.zeros(rows.shape, jnp.float32)
+    late[...] = jnp.zeros(late.shape, jnp.float32)
+    pick_t[...] = (col_id == jnp.where(row_id < 128, 2 * row_id, 2 * row_id - 255)).astype(jnp.float32).astype(jnp.bfloat16)
     for c in range(3):
         widen_own(0, c, range(4, 12))
     copies[4].wait()
@@ -459,7 +459,7 @@
             device_id=target, device_id_type=MESH,
         )
 
-    for d in range(1, n_lat):
+    for d in sorted(range(1, n_lat), key=lambda d: -min(d, n_lat - d)):
         row_copy(0, d).start()
     for j in range(n_steps - DEPTH + 1, n_steps + 1):
         put_out(j - 1)
@@ -469,7 +469,7 @@
     for d in range(1, n_lat):
         total = total + row_lat[d]
     row_rad[rad] = total
-    for d in range(1, n_rad):
+    for d in sorted(range(1, n_rad), key=lambda d: -min(d, n_rad - d)):
         row_copy(1, d).start()
     each_direction(False, lambda n: eta_copy(n).wait_send())
     for e in range(n_exchange):
@@ -482,23 +482,23 @@
     total = row_rad[0]
     for d in range(1, n_rad):
         total = total + row_rad[d]
-    total = total * (1.0 / dof_count)
-    for i in range(width):
-        line = total if i == 0 else pltpu.roll(jnp.broadcast_to(total, (8, 128)), 128 - i * width, 1)[0:1]
-        gram[i : i + 1, :] = line[:, :width]
+    gram[...] = total
     for d in range(1, n_rad):
         row_copy(1, d).wait_send()
 
 
-def leave(vectors, sums, new_basis, gram, sems):
-    copies = [
-        pltpu.make_async_copy(vectors, new_basis, sems.at[0]),
-        pltpu.make_async_copy(sums, gram, sems.at[1]),
-    ]
-    for copy in copies:
-        copy.start()
-    for copy in copies:
-        copy.wait()
+def leave(dof_count, vectors, sums, new_basis, gram, square, sems):
+    away = pltpu.make_async_copy(vectors, new_basis, sems.at[0])
+    away.start()
+    total = jnp.broadcast_to(sums[...] * (1.0 / dof_count), (8, 128))
+    width = square.shape[0]
+    for i in range(width):
+        line = total if i == 0 else pltpu.roll(total, 128 - i * width, 1)
+        square[i : i + 1, :] = line[0:1, :width]
+    last = pltpu.make_async_copy(square, gram, sems.at[1])
+    last.start()
+    away.wait()
+    last.wait()
 
 
 def solution(mesh):
@@ -515,11 +515,11 @@
         dma = pltpu.SemaphoreType.DMA
         vectors, sums = pl.pallas_call(
             functools.partial(
-                kernel, n_steps, n_prev, viscosity.shape[0], n_rad, n_lat, dof_count
+                kernel, n_steps, n_prev, viscosity.shape[0], n_rad, n_lat
             ),
             out_shape=(
                 jax.ShapeDtypeStruct((n_steps,) + residual.shape, f32),
-                jax.ShapeDtypeStruct((width, width), f32),
+                jax.ShapeDtypeStruct((1, 128), f32),
             ),
             in_specs=[pl.BlockSpec(memory_space=pltpu.HBM)] * 5,
             out_specs=(
@@ -559,14 +559,14 @@
         )(*(pltpu.with_memory_space_constraint(x, pltpu.HBM) for x in (residual, prev_basis, layer_ids, viscosity, shifts)))
 
         return pl.pallas_call(
-            leave,
+            functools.partial(leave, dof_count),
             out_shape=(
                 jax.ShapeDtypeStruct(vectors.shape, f32),
-                jax.ShapeDtypeStruct(sums.shape, f32),
+                jax.ShapeDtypeStruct((width, width), f32),
             ),
             in_specs=[pl.BlockSpec(memory_space=pltpu.VMEM)] * 2,
             out_specs=(pl.BlockSpec(memory_space=pltpu.HBM), pl.BlockSpec(memory_space=pltpu.HBM)),
-            scratch_shapes=[dma((2,))],
+            scratch_shapes=[pltpu.VMEM((width, width), f32), dma((2,))],
             compiler_params=pltpu.CompilerParams(vmem_limit_bytes=2**20),
         )(vectors, sums)
 

time: 34.2 us -> 34.2 us (level)
  no operation moved by 1% of the time
where the time goes in v3:
time: 34.2 us; the launch traced here: 34.1 us
  Pallas kernels  33.4 us (98%)
  between operations  0.64 us (2%)
    pallas_call x1, Pallas kernels, on_device(): pl.pallas_call(functools.partial(kernel, n_steps, n_prev, viscosity.shape...  32.5 us
    pallas_call x1, Pallas kernels, on_device(): pl.pallas_call(functools.partial(leave, dof_count), out_shape=(jax.ShapeD...  0.9 us

profile of v3, /device:TPU:1, one launch (start us, length us, event | category | flops | bytes accessed | tf_op | source)
XLA Modules:
  0.0 34.1 jit_solution(14534566914677109011)
XLA Ops:
  0.6 32.5 %shard_map.68 = (f32[4,3,8,8,256]{4,3,2,1,0:T(8,128)S(1)}, f32[1,128]{1,0:T(1,128)S(1)}) custom-call(f32[3,8,8,256]{3,2,1,0:T(8,128)} %residual.1, f32[4,3,8,8,256]{4,3,2,1,0:T(8,128)} %prev_basis.1, s32[4,4,128]{2,1,0:T(4,128)} %layer_ids.1, f32[8]{0:T(128)} %viscosity_in.1, f32[4]{0:T(128)} %shifts_in.1), custom_call_target="tpu_custom_call" | custom-call | tf_op jit(solution)/shard_map/pallas_call | solution.py:516
  33.2 0.9 %shard_map.69 = (f32[4,3,8,8,256]{4,3,2,1,0:T(8,128)}, f32[9,9]{1,0:T(8,128)}) custom-call(f32[4,3,8,8,256]{4,3,2,1,0:T(8,128)S(1)} %get-tuple-element.4.vectors, f32[1,128]{1,0:T(1,128)S(1)} %get-tuple-element.5.sums), custom_call_target="tpu_custom_call" | custom-call | tf_op jit(solution)/shard_map/pallas_call | solution.py:561

commit v4 on v3

--- a/solution.py
+++ b/solution.py
@@ -156,7 +156,7 @@
             pack[e, c, 0, p] = jnp.where(upper_rows, even, pltpu.roll(odd, 4, 0))
             pack[e, c, 1, p] = jnp.where(upper_rows, pltpu.roll(even, 4, 0), odd)
 
-    def halo_copy(e, c, n):
+    def halo_copy(e, c, n, way=1):
         dr, dl = DIRECTIONS[n]
         k = e * DEPTH
         source, target, size = {
@@ -170,17 +170,17 @@
             dst = side.at[e, c, 1 if dl < 0 else 0, pl.ds(target, size)]
         return pltpu.make_async_remote_copy(
             src_ref=src, dst_ref=dst, send_sem=send_sem.at[e, c, n], recv_sem=recv_sem.at[e, c, n],
-            device_id={"lat": lat + dl, "rad": rad + dr}, device_id_type=MESH,
+            device_id={"lat": lat + way * dl, "rad": rad + way * dr}, device_id_type=MESH,
         )
 
-    def eta_copy(n):
+    def eta_copy(n, way=1):
         dr, dl = DIRECTIONS[n]
         source, target, size = {1: (1, 0, 1), -1: (0, 3, 1), 0: (0, 1, 2)}[dr]
         return pltpu.make_async_remote_copy(
             src_ref=eta.at[1, pl.ds(1 + source, size)],
             dst_ref=eta.at[1 - dl, pl.ds(target, size)],
             send_sem=esend_sem.at[n], recv_sem=erecv_sem.at[n],
-            device_id={"lat": lat + dl, "rad": rad + dr}, device_id_type=MESH,
+            device_id={"lat": lat + way * dl, "rad": rad + way * dr}, device_id_type=MESH,
         )
 
     def each_direction(receive, act, which=range(8)):
@@ -391,7 +391,7 @@
         dots(m)
     hear(0)
     tell(1)
-    each_direction(True, lambda n: eta_copy(n).wait_recv())
+    each_direction(True, lambda n: eta_copy(n, -1).wait_recv())
     for h in range(4):
         own = eta[1, h]
         beside = jnp.where(sub % 4 < 2, eta[2, h], eta[0, h])
@@ -408,7 +408,7 @@
         final = e == n_exchange - 1
 
         def component(c, nothing):
-            each_direction(True, lambda n: halo_copy(e, c, n).wait_recv())
+            each_direction(True, lambda n: halo_copy(e, c, n, -1).wait_recv())
             widen_own(k, c, list(range(low, 4)) + list(range(12, high)))
             widen_sides(e, c, range(low, high))
             for step in range(DEPTH):

time: 34.2 us -> 34.2 us (level)
  no operation moved by 1% of the time
where the time goes in v4:
time: 34.2 us; the launch traced here: 34.1 us
  Pallas kernels  33.4 us (98%)
  between operations  0.64 us (2%)
    pallas_call x1, Pallas kernels, on_device(): pl.pallas_call(functools.partial(kernel, n_steps, n_prev, viscosity.shape...  32.5 us
    pallas_call x1, Pallas kernels, on_device(): pl.pallas_call(functools.partial(leave, dof_count), out_shape=(jax.ShapeD...  0.9 us

profile of v4, /device:TPU:1, one launch (start us, length us, event | category | flops | bytes accessed | tf_op | source)
XLA Modules:
  0.0 34.1 jit_solution(14534566914677109011)
XLA Ops:
  0.6 32.5 %shard_map.68 = (f32[4,3,8,8,256]{4,3,2,1,0:T(8,128)S(1)}, f32[1,128]{1,0:T(1,128)S(1)}) custom-call(f32[3,8,8,256]{3,2,1,0:T(8,128)} %residual.1, f32[4,3,8,8,256]{4,3,2,1,0:T(8,128)} %prev_basis.1, s32[4,4,128]{2,1,0:T(4,128)} %layer_ids.1, f32[8]{0:T(128)} %viscosity_in.1, f32[4]{0:T(128)} %shifts_in.1), custom_call_target="tpu_custom_call" | custom-call | tf_op jit(solution)/shard_map/pallas_call | solution.py:516
  33.2 0.9 %shard_map.69 = (f32[4,3,8,8,256]{4,3,2,1,0:T(8,128)}, f32[9,9]{1,0:T(8,128)}) custom-call(f32[4,3,8,8,256]{4,3,2,1,0:T(8,128)S(1)} %get-tuple-element.4.vectors, f32[1,128]{1,0:T(1,128)S(1)} %get-tuple-element.5.sums), custom_call_target="tpu_custom_call" | custom-call | tf_op jit(solution)/shard_map/pallas_call | solution.py:561
